TPU v7x, 8 devices: a whole 2x2x1 slice. The times are simulated.
8 devices in a mesh: data: 8 (over z, y, x, core).
Axes of the slice: x: 2, y: 2, z: 1, core: 2. Of those that a mesh axis runs over, the one named last changes fastest.
Arguments:
- x_act: bfloat16 [128, 196, 384], P('data')
- y_tgt: bfloat16 [128, 196, 384], P('data')
- w_in: float32 [12, 384, 1536], replicated
- w_out: float32 [12, 1536, 384], replicated
Outputs:
- output 1: float32 [12, 384, 1536], replicated
- output 2: float32 [12, 1536, 384], replicated
- output 3: float32 [], replicated
All inputs are finite; a program needn't handle non-finite values.
Results may differ from a plain program's by a relative error of at most 0.00259924.
Values are sent between devices in bfloat16 or wider.
A program may use at most 1 GiB of HBM per device.

v0:
```python
import math
import jax
import jax.numpy as jnp
from jax import lax
from jax.sharding import PartitionSpec as P

RHO_FRAC = 0.1
LEARN_RATE = 1.0
MICRO_STEPS = 2


def gelu_tanh(z_val):
    return jax.nn.gelu(z_val, approximate=True)


def layer_forward(h_act, wi_cast, wo_cast):
    z_pre = jnp.einsum("bsd,df->bsf", h_act, wi_cast, preferred_element_type=jnp.float32).astype(jnp.bfloat16)
    gelu_out = gelu_tanh(z_pre.astype(jnp.float32)).astype(jnp.bfloat16)
    u_out = jnp.einsum("bsf,fd->bsd", gelu_out, wo_cast, preferred_element_type=jnp.float32)
    return (h_act.astype(jnp.float32) + u_out).astype(jnp.bfloat16), z_pre


def micro_grads(x_mb, y_mb, wi_list, wo_list):
    n_layers = len(wi_list)
    h_list = [x_mb]
    z_list = []
    for layer_idx in range(n_layers):
        h_next, z_pre = layer_forward(h_list[-1], wi_list[layer_idx], wo_list[layer_idx])
        h_list.append(h_next)
        z_list.append(z_pre)
    out_err = h_list[-1].astype(jnp.float32) - y_mb.astype(jnp.float32)
    sq_sum = jnp.sum(out_err * out_err)
    back_grad = out_err.astype(jnp.bfloat16)
    sums_in = [None] * n_layers
    sums_out = [None] * n_layers
    for layer_idx in reversed(range(n_layers)):
        gelu_out, gelu_vjp = jax.vjp(gelu_tanh, z_list[layer_idx].astype(jnp.float32))
        sums_out[layer_idx] = jnp.einsum("bsf,bsd->fd", gelu_out.astype(jnp.bfloat16), back_grad, preferred_element_type=jnp.float32)
        d_act = jnp.einsum("bsd,fd->bsf", back_grad, wo_list[layer_idx], preferred_element_type=jnp.float32)
        d_pre = gelu_vjp(d_act)[0].astype(jnp.bfloat16)
        sums_in[layer_idx] = jnp.einsum("bsd,bsf->df", h_list[layer_idx], d_pre, preferred_element_type=jnp.float32)
        if layer_idx > 0:
            back_in = jnp.einsum("bsf,df->bsd", d_pre, wi_list[layer_idx], preferred_element_type=jnp.float32)
            back_grad = (back_grad.astype(jnp.float32) + back_in).astype(jnp.bfloat16)
    return sums_in, sums_out, sq_sum


def grad_pass(x_loc, y_loc, wi_list, wo_list):
    mb_rows = x_loc.shape[0] // MICRO_STEPS
    sums_in, sums_out, sq_sum = micro_grads(x_loc[:mb_rows], y_loc[:mb_rows], wi_list, wo_list)
    for micro_idx in range(1, MICRO_STEPS):
        row_lo = micro_idx * mb_rows
        more_in, more_out, more_sq = micro_grads(x_loc[row_lo:row_lo + mb_rows], y_loc[row_lo:row_lo + mb_rows], wi_list, wo_list)
        sums_in = [left_sum + right_sum for left_sum, right_sum in zip(sums_in, more_in)]
        sums_out = [left_sum + right_sum for left_sum, right_sum in zip(sums_out, more_out)]
        sq_sum = sq_sum + more_sq
    return sums_in, sums_out, sq_sum


def solution(mesh):
    n_dev = mesh.shape["data"]

    def local_step(x_loc, y_loc, w_in, w_out):
        n_layers, d_model, d_ff = w_in.shape
        tok_scale = 1.0 / (x_loc.shape[0] * n_dev * x_loc.shape[1] * d_model)
        rho_val = RHO_FRAC * math.sqrt(n_layers * (d_model + d_ff))
        wi_cast = [w_in[layer_idx].astype(jnp.bfloat16) for layer_idx in range(n_layers)]
        wo_cast = [w_out[layer_idx].astype(jnp.bfloat16) for layer_idx in range(n_layers)]
        sums_in, sums_out, _ = grad_pass(x_loc, y_loc, wi_cast, wo_cast)
        grad_in = [lax.psum(part_sum, "data") * tok_scale for part_sum in sums_in]
        grad_out = [lax.psum(part_sum, "data") * tok_scale for part_sum in sums_out]
        sq_norm = sum(jnp.sum(grad_mat * grad_mat) for grad_mat in grad_in + grad_out)
        perturb_coef = rho_val / jnp.sqrt(sq_norm)
        pi_cast = [(w_in[layer_idx] + perturb_coef * grad_in[layer_idx]).astype(jnp.bfloat16) for layer_idx in range(n_layers)]
        po_cast = [(w_out[layer_idx] + perturb_coef * grad_out[layer_idx]).astype(jnp.bfloat16) for layer_idx in range(n_layers)]
        second_in, second_out, second_sq = grad_pass(x_loc, y_loc, pi_cast, po_cast)
        total_in = [lax.psum(part_sum, "data") for part_sum in second_in]
        total_out = [lax.psum(part_sum, "data") for part_sum in second_out]
        total_sq = lax.psum(second_sq, "data")
        new_in = jnp.stack([w_in[layer_idx] - LEARN_RATE * (total_in[layer_idx] * tok_scale) for layer_idx in range(n_layers)])
        new_out = jnp.stack([w_out[layer_idx] - LEARN_RATE * (total_out[layer_idx] * tok_scale) for layer_idx in range(n_layers)])
        pert_loss = 0.5 * (total_sq * tok_scale)
        return new_in, new_out, pert_loss

    return jax.shard_map(local_step, mesh=mesh, in_specs=(P("data"), P("data"), P(), P()), out_specs=(P(), P(), P()), check_vma=False)
```

profile of v0, /device:TPU:0, one launch (start us, length us, event | category | flops | bytes accessed | tf_op | source)
XLA Modules:
  0.0 3460.7 jit_solution(13112108499473781972)
XLA Ops:
  12.2 12.0 fusion.607
  32.0 12.9 fusion.605
  45.0 8.4 fusion.533
  137.5 8.2 fusion.128
  157.5 8.3 fusion.131
  177.7 8.5 fusion.134
  218.4 8.2 fusion.140
  238.6 8.3 fusion.143
  258.8 8.5 fusion.146
  299.6 8.2 fusion.152
  319.8 8.3 fusion.155
  340.0 8.5 fusion.158
  360.6 13.8 convolution_bitcast_fusion.94
  468.6 8.3 fusion.164
  693.7 14.4 fusion.481
  708.1 9.0 fusion.493
  717.2 940.7 %all-reduce.7.cloned.1.call-done = (f32[384,1536]{1,0:T(8,128)}, f32[384,1536]{1,0:T(8,128)}, f32[384,1536]{1,0:T(8,128)}, f32[384,1536]{1,0:T(8,128)}, f32[384,...) async-done(((f32[384,1536]{1,0:T(8,128)}, ...) | async-done | bytes 56623120 | tf_op jit(solution)/shard_map/psum | solution.py:70
  1715.6 17.8 fusion.608
  1733.4 19.2 fusion.606
  1862.8 9.5 fusion.62
  1924.8 8.2 fusion.71
  1945.0 8.3 fusion.74
  1965.2 8.5 fusion.77
  2005.8 8.2 fusion.83
  2026.1 8.3 fusion.86
  2046.3 8.5 fusion.89
  2082.7 13.5 convolution_bitcast_fusion.46
  2096.3 8.4 convolution_bitcast_fusion.22
  2418.0 14.3 fusion.506
  2432.3 9.1 fusion.518
  2442.6 23.8 psum.391
  2467.1 914.3 %all-reduce.5.cloned.1.call-done = (f32[384,1536]{1,0:T(8,128)}, f32[384,1536]{1,0:T(8,128)}, f32[384,1536]{1,0:T(8,128)}, f32[384,1536]{1,0:T(8,128)}, f32[384,...) async-done(((f32[384,1536]{1,0:T(8,128)}, ...) | async-done | bytes 56623120 | tf_op jit(solution)/shard_map/psum | solution.py:77
  (1167 shorter events, 1246.7 us)
Async XLA Ops:
  7.2 1650.8 %all-reduce.7.cloned.1.call-start = ((), (), s32[]{:S(2)}) async-start(), calls=%async_computation.1 | async-start | bytes 113246208 | tf_op jit(solution)/shard_map/psum | solution.py:70
  10.3 34.7 %copy-start.121 = (bf16[8,196,384]{2,0,1:T(8,128)(2,1)}, bf16[8,196,384]{2,0,1:T(8,128)(2,1)S(1)}, u32[]{:S(2)}) copy-start(bf16[8,196,384]{2,0,1:T(8,128)(2,1)S(1)} %get-tuple-element.101) | copy-start | bytes 3612676
  24.2 29.2 copy-start.154
  24.2 36.3 %copy-start.169 = (bf16[384,1536,1]{1,0,2:T(8,128)(2,1)}, bf16[384,1536,1]{1,0,2:T(8,128)(2,1)S(1)}, u32[]{:S(2)}) copy-start(bf16[384,1536,1]{1,0,2:T(8,128)(2,1)S(1)} %get-tuple-element.83) | copy-start | bytes 3538948
  24.2 43.6 %copy-start.185 = (bf16[384,1536,1]{1,0,2:T(8,128)(2,1)}, bf16[384,1536,1]{1,0,2:T(8,128)(2,1)S(1)}, u32[]{:S(2)}) copy-start(bf16[384,1536,1]{1,0,2:T(8,128)(2,1)S(1)} %get-tuple-element.82) | copy-start | bytes 3538948
  24.2 50.7 %copy-start.201 = (bf16[384,1536,1]{1,0,2:T(8,128)(2,1)}, bf16[384,1536,1]{1,0,2:T(8,128)(2,1)S(1)}, u32[]{:S(2)}) copy-start(bf16[384,1536,1]{1,0,2:T(8,128)(2,1)S(1)} %get-tuple-element.81) | copy-start | bytes 3538948
  24.2 57.7 %copy-start.213 = (bf16[384,1536,1]{1,0,2:T(8,128)(2,1)}, bf16[384,1536,1]{1,0,2:T(8,128)(2,1)S(1)}, u32[]{:S(2)}) copy-start(bf16[384,1536,1]{1,0,2:T(8,128)(2,1)S(1)} %get-tuple-element.80) | copy-start | bytes 3538948
  44.9 25.8 copy-start.209
  44.9 32.9 copy-start.221
  172.5 20.4 slice-start.71
  253.6 20.5 slice-start.47
  334.8 20.4 slice-start.7
  549.8 20.4 slice-start.45
  570.2 20.6 slice-start.35
  611.2 20.4 slice-start.19
  631.6 20.4 slice-start.15
  651.9 20.5 slice-start.11
  717.2 2664.2 %all-reduce.5.cloned.1.call-start = ((), (), s32[]{:S(2)}) async-start(), calls=%async_computation | async-start | bytes 113246208 | tf_op jit(solution)/shard_map/psum | solution.py:77
  1733.4 39.4 %copy-start.127 = (bf16[1536,384,1]{1,0,2:T(8,128)(2,1)}, bf16[1536,384,1]{1,0,2:T(8,128)(2,1)S(1)}, u32[]{:S(2)}) copy-start(bf16[1536,384,1]{1,0,2:T(8,128)(2,1)S(1)} %get-tuple-element.52) | copy-start | bytes 3538948
  1759.1 70.9 %copy-start.247 = (bf16[1536,384,1]{1,0,2:T(8,128)(2,1)}, bf16[1536,384,1]{1,0,2:T(8,128)(2,1)S(1)}, u32[]{:S(2)}) copy-start(bf16[1536,384,1]{1,0,2:T(8,128)(2,1)S(1)} %get-tuple-element.73) | copy-start | bytes 3538948
  1759.1 125.6 %copy-start.274 = (bf16[1536,384,1]{1,0,2:T(8,128)(2,1)}, bf16[1536,384,1]{1,0,2:T(8,128)(2,1)S(1)}, u32[]{:S(2)}) copy-start(bf16[1536,384,1]{1,0,2:T(8,128)(2,1)S(1)} %get-tuple-element.72) | copy-start | bytes 3538948
  1759.1 145.5 %copy-start.264 = (bf16[1536,384,1]{1,0,2:T(8,128)(2,1)}, bf16[1536,384,1]{1,0,2:T(8,128)(2,1)S(1)}, u32[]{:S(2)}) copy-start(bf16[1536,384,1]{1,0,2:T(8,128)(2,1)S(1)} %get-tuple-element.74) | copy-start | bytes 3538948
  1765.3 61.8 %copy-start.255 = (bf16[384,1536,1]{1,0,2:T(8,128)(2,1)}, bf16[384,1536,1]{1,0,2:T(8,128)(2,1)S(1)}, u32[]{:S(2)}) copy-start(bf16[384,1536,1]{1,0,2:T(8,128)(2,1)S(1)} %get-tuple-element.70) | copy-start | bytes 3538948
  1765.3 127.4 %copy-start.278 = (bf16[384,1536,1]{1,0,2:T(8,128)(2,1)}, bf16[384,1536,1]{1,0,2:T(8,128)(2,1)S(1)}, u32[]{:S(2)}) copy-start(bf16[384,1536,1]{1,0,2:T(8,128)(2,1)S(1)} %get-tuple-element.69) | copy-start | bytes 3538948
  1765.4 147.5 %copy-start.270 = (bf16[384,1536,1]{1,0,2:T(8,128)(2,1)}, bf16[384,1536,1]{1,0,2:T(8,128)(2,1)S(1)}, u32[]{:S(2)}) copy-start(bf16[384,1536,1]{1,0,2:T(8,128)(2,1)S(1)} %get-tuple-element.71) | copy-start | bytes 3538948
  1959.9 20.4 slice-start.49
  2041.1 20.5 slice-start.21
  2274.2 20.5 slice-start.43
  2355.7 20.6 slice-start.13
  3400.3 29.3 slice-start
  3404.0 25.7 slice-start.1
  3407.6 22.0 slice-start.2
  (387 other events, 2515.0 us)
Sparse Core Ops, SparseCore 0:
  717.3 940.5 all-reduce.6
  2441.5 939.8 all-reduce.4
where the time goes:
time: 3470 us; the launch traced here: 3460 us
  waiting for transfers between devices  1860 us (54%)
  matrix products  1340 us (39%)
  other arithmetic  158 us (5%)
  local copies, waits for them, and re-layouts  42.7 us (1%)
  between operations  39.7 us (1%)
    psum x1, waiting for transfers between devices, local_step(): grad_in = [lax.psum(part_sum, 'data') * tok_scale for part_sum in sums_in]  941 us
    psum x1, waiting for transfers between devices, local_step(): total_in = [lax.psum(part_sum, 'data') for part_sum in second_in]  914 us
    dot_general x44, matrix products, micro_grads(): jnp.einsum('bsd,fd->bsf', back_grad, wo_list[layer_idx], preferred_elemen...  361 us
    dot_general x48, matrix products, micro_grads(): jnp.einsum('bsf,bsd->fd', gelu_out.astype(jnp.bfloat16), back_grad, prefe...  272 us
    dot_general x48, matrix products, micro_grads(): jnp.einsum('bsd,bsf->df', h_list[layer_idx], d_pre, preferred_element_typ...  222 us
    dot_general x48, matrix products, layer_forward(): jnp.einsum('bsf,fd->bsd', gelu_out, wo_cast, preferred_element_type=jnp.f...  209 us
    dot_general x48, matrix products, layer_forward(): jnp.einsum('bsd,df->bsf', h_act, wi_cast, preferred_element_type=jnp.floa...  148 us
    dot_general x44, matrix products, micro_grads(): jnp.einsum('bsf,df->bsd', d_pre, wi_list[layer_idx], preferred_element_ty...  131 us
  transfers between devices with their start and end apart: 2, of which 2 were waited for; matrix products, arithmetic and copies ran while one was open for 0% of the time, Pallas kernels for 0%

commit v1 on v0

v1 whole, which is shorter than its diff:
```python
import functools
import math

import jax
import jax.numpy as jnp
from jax import lax
from jax.experimental import pallas as pl
from jax.experimental.pallas import tpu as pltpu
from jax.sharding import PartitionSpec as P

RHO_FRAC = 0.1
LEARN_RATE = 1.0
N_TILES = 4
GELU_C0 = math.sqrt(2.0 / math.pi)
GELU_C1 = GELU_C0 * 0.044715
BF = jnp.bfloat16
F32 = jnp.float32
MESH = pl.DeviceIdType.MESH
ANY = pl.ANY
VMEM_BYTES = 67043328
D2D, P1, P2, G2, G1, GD = range(6)


def dot(left, right, left_dim, right_dim):
    return lax.dot_general(left, right, (((left_dim,), (right_dim,)), ((), ())), preferred_element_type=F32)


def gelu(z):
    th = jnp.tanh(z * (z * z * GELU_C1 + GELU_C0))
    half = 0.5 * z
    return half * th + half


def gelu_and_slope(z):
    sq = z * z
    th = jnp.tanh(z * (sq * GELU_C1 + GELU_C0))
    half = 0.5 * z
    up = th + 1.0
    bend = (half * (1.0 - th)) * (sq * (3.0 * GELU_C1) + GELU_C0)
    return half * up, up * (bend + 0.5)


def place():
    me = lax.axis_index("data")
    core, cx, cy = lax.rem(me, 2), lax.rem(me // 2, 2), me // 4
    return me, core, cx, cy, me + 1 - 2 * core, me + 2 - 4 * cx, me + 4 - 8 * cy


def greet(peers):
    barrier = pltpu.get_barrier_semaphore()
    for peer in peers:
        pl.semaphore_signal(barrier, inc=1, device_id=(peer,), device_id_type=MESH)
    pl.semaphore_wait(barrier, len(peers))


def remote(src, dst, send_sem, recv_sem, peer):
    return pltpu.make_async_remote_copy(src_ref=src, dst_ref=dst, send_sem=send_sem, recv_sem=recv_sem,
                                        device_id=(peer,), device_id_type=MESH)


def share_copies(me, gath, send, recv):
    return [remote(gath.at[me], gath.at[me], send.at[k], recv.at[k], lax.rem(me + k + 1, 8)) for k in range(7)]


def fold_rows(err, d_model):
    sq = err * err
    part = jnp.sum(sq.reshape(sq.shape[0] // 8, 8, d_model), axis=0)
    return part[:, :128] + part[:, 128:256] + part[:, 256:]


def forward_tile(rows, wi, wo, z_ref, h_ref, err_ref, loss_ref, y_ref, h_all, a_s, last):
    h = h_all[rows, :]
    h_ref[0] = h
    z = dot(h, wi, 1, 0).astype(BF)
    z_ref[0] = z
    a_s[...] = gelu(z.astype(F32)).astype(BF)
    u = dot(a_s[...], wo, 1, 0)
    h_next = (h.astype(F32) + u).astype(BF)
    h_all[rows, :] = h_next

    @pl.when(last)
    def _():
        err = h_next.astype(F32) - y_ref[...].astype(F32)
        err_ref[rows, :] = err.astype(BF)
        loss_ref[...] += fold_rows(err, err.shape[1])


def forward_kernel(x_ref, y_ref, wi_ref, wo_ref, z_ref, h_ref, err_ref, loss_ref, vi_ref, vo_ref, h_all, a_s):
    layer, tile = pl.program_id(0), pl.program_id(1)
    rows = pl.ds(tile * a_s.shape[0], a_s.shape[0])

    @pl.when(layer == 0)
    def _():
        h_all[rows, :] = x_ref[...]

    @pl.when((layer == 0) & (tile == 0))
    def _():
        loss_ref[...] = jnp.zeros_like(loss_ref)

    @pl.when(tile == 0)
    def _():
        vi_ref[0] = wi_ref[0].astype(BF)
        vo_ref[0] = wo_ref[0].astype(BF)

    forward_tile(rows, vi_ref[0], vo_ref[0], z_ref, h_ref, err_ref, loss_ref, y_ref, h_all, a_s,
                 layer == pl.num_programs(0) - 1)


def gather_kernel(n_layers, rho, x_ref, y_ref, sq_ref, g_hbm, wi_hbm, wo_hbm, z_ref, h_ref, err_ref, loss_ref, vi_ref, vo_ref,
                  h_all, a_s, v_buf, g_own, w_own, gath, load_sem, share_send, share_recv, send, recv):
    layer, tile = pl.program_id(0), pl.program_id(1)
    me, core, cx, cy, mate, nx, ny = place()
    d = g_own.shape[-1]
    half = d // 2
    rows = pl.ds(tile * a_s.shape[0], a_s.shape[0])
    row_a = pl.multiple_of(half * cy, half)
    row_b = pl.multiple_of(half * cx, half)

    def at_a(k):
        return v_buf.at[k, core, cx, pl.ds(row_a, half), :]

    def at_b(k):
        return v_buf.at[k, core, 2 + cy, pl.ds(row_b, half), :]

    def copies(stage, k):
        def one(ref, link, peer):
            return remote(ref, ref, send.at[stage - G2, link, k], recv.at[stage - G2, link, k], peer)

        if stage == G2:
            return [one(at_a(k), 0, ny), one(at_b(k), 1, nx)]
        if stage == G1:
            return [one(v_buf.at[k, core, cx], 0, nx), one(v_buf.at[k, core, 2 + cy], 1, ny)]
        return [one(v_buf.at[k, core], 0, mate)]

    def start(stage, k):
        for copy in copies(stage, k):
            copy.start()

    def wait(stage, k):
        for copy in copies(stage, k):
            copy.wait()

    @pl.when((layer == 0) & (tile == 0))
    def _():
        loss_ref[...] = jnp.zeros_like(loss_ref)
        load_g = pltpu.make_async_copy(g_hbm, g_own, load_sem.at[0])
        load_g.start()

        @pl.when(core == 0)
        def _():
            for k in range(n_layers):
                pltpu.make_async_copy(wi_hbm.at[k, pl.ds(row_a, half), pl.ds(pl.multiple_of(d * cx, d), d)],
                                      w_own.at[k, 0], load_sem.at[1]).start()
                pltpu.make_async_copy(wi_hbm.at[k, pl.ds(row_b, half), pl.ds(pl.multiple_of(d * (2 + cy), d), d)],
                                      w_own.at[k, 1], load_sem.at[1]).start()

        @pl.when(core == 1)
        def _():
            for k in range(n_layers):
                pltpu.make_async_copy(wo_hbm.at[k, pl.ds(pl.multiple_of(d * cx + row_a, half), half), :],
                                      w_own.at[k, 0], load_sem.at[1]).start()
                pltpu.make_async_copy(wo_hbm.at[k, pl.ds(pl.multiple_of(d * (2 + cy) + row_b, half), half), :],
                                      w_own.at[k, 1], load_sem.at[1]).start()

        greet([lax.rem(me + k + 1, 8) for k in range(7)])
        gath[me] = sq_ref[...]
        shares = share_copies(me, gath, share_send, share_recv)
        for copy in shares:
            copy.start()
        load_g.wait()
        pltpu.make_async_copy(g_hbm, w_own, load_sem.at[1]).wait()
        for copy in shares:
            copy.wait()
        total = jnp.sum(gath[...])
        coef = rho / jnp.sqrt(jnp.full((1, d), total, F32))

        def perturb(k, carry):
            at_a(k)[...] = (w_own[k, 0] + coef * g_own[k, 0]).astype(BF)
            at_b(k)[...] = (w_own[k, 1] + coef * g_own[k, 1]).astype(BF)
            return carry

        lax.fori_loop(0, n_layers, perturb, 0)
        start(G2, 0)
        start(G2, 1)
        wait(G2, 0)
        start(G1, 0)
        wait(G2, 1)
        start(G2, 2)
        wait(G1, 0)
        start(GD, 0)
        start(G1, 1)

    @pl.when(tile == 0)
    def _():
        @pl.when(layer + 1 < n_layers)
        def _():
            wait(G1, layer + 1)

        wait(GD, layer)

        @pl.when(layer + 1 < n_layers)
        def _():
            start(GD, layer + 1)

        @pl.when(layer + 2 < n_layers)
        def _():
            wait(G2, layer + 2)
            start(G1, layer + 2)

        @pl.when(layer + 3 < n_layers)
        def _():
            start(G2, layer + 3)

        for blk in range(4):
            vi_ref[0, :, blk * d:(blk + 1) * d] = v_buf[layer, 0, blk]
            vo_ref[0, blk * d:(blk + 1) * d, :] = v_buf[layer, 1, blk]

    @pl.when(layer == 0)
    def _():
        h_all[rows, :] = x_ref[...]

    forward_tile(rows, vi_ref[0], vo_ref[0], z_ref, h_ref, err_ref, loss_ref, y_ref, h_all, a_s, layer == n_layers - 1)


def backward_kernel(full, n_layers, scale, *refs):
    n_in = 8 if full else 5
    n_out = 3 if full else 2
    ins, outs, scr = refs[:n_in], refs[n_in:n_in + n_out], list(refs[n_in + n_out:])
    q_ref, z_ref, h_ref, vi_ref, vo_ref = ins[:5]
    q_s, acc_i, acc_o, a_s, p_s, s_buf, rd, rp1, rp2, send, recv, q_sem = scr[:12]
    step, tile = pl.program_id(0), pl.program_id(1)
    me, core, cx, cy, mate, nx, ny = place()
    d = rd.shape[-1]
    half = d // 2
    tok = a_s.shape[0]
    keep_a = pl.ds(pl.multiple_of(half * cy, half), half)
    give_a = pl.ds(pl.multiple_of(half * (1 - cy), half), half)
    keep_b = pl.ds(pl.multiple_of(half * cx, half), half)
    give_b = pl.ds(pl.multiple_of(half * (1 - cx), half), half)
    if full:
        loss_ref, wi_hbm, wo_hbm = ins[5:]
        wi_new, wo_new, loss_out = outs
        tot, w_i, w_o, gath, share_send, share_recv, load_sem, store_sem = scr[12:]
    else:
        g_out, sq_out = outs
        own, own_sem = scr[12:]

    def copies(stage, k):
        par, par3 = lax.rem(k, 2), lax.rem(k, 3)

        def one(src, dst, link, peer):
            return remote(src, dst, send.at[stage, link, par], recv.at[stage, link, par], peer)

        if stage == D2D:
            return [one(s_buf.at[1 - core], rd.at[par3], 0, mate)]
        if stage == P1:
            return [one(rd.at[par3, 1 - cx], rp1.at[par, 0], 0, nx), one(rd.at[par3, 3 - cy], rp1.at[par, 1], 1, ny)]
        if stage == P2:
            return [one(rd.at[par3, cx, give_a, :], rp2.at[par, 0], 0, ny),
                    one(rd.at[par3, 2 + cy, give_b, :], rp2.at[par, 1], 1, nx)]
        if stage == G2:
            part_a, part_b = tot.at[par3, core, cx, keep_a, :], tot.at[par3, core, 2 + cy, keep_b, :]
            return [one(part_a, part_a, 0, ny), one(part_b, part_b, 1, nx)]
        if stage == G1:
            part_a, part_b = tot.at[par3, core, cx], tot.at[par3, core, 2 + cy]
            return [one(part_a, part_a, 0, nx), one(part_b, part_b, 1, ny)]
        whole = tot.at[par3, core]
        return [one(whole, whole, 0, mate)]

    def start(stage, k):
        for copy in copies(stage, k):
            copy.start()

    def wait(stage, k):
        for copy in copies(stage, k):
            copy.wait()

    def when_layer(lag, body):
        @pl.when((step >= lag) & (step - lag < n_layers))
        def _():
            body(step - lag)

    def finish_pair(k):
        wait(D2D, k)
        par3 = lax.rem(k, 3)
        for blk in range(4):
            rd[par3, blk] += s_buf[core, blk]
        start(P1, k)

    def finish_p1(k):
        wait(P1, k)
        par, par3 = lax.rem(k, 2), lax.rem(k, 3)
        rd[par3, cx] += rp1[par, 0]
        rd[par3, 2 + cy] += rp1[par, 1]
        start(P2, k)

    def owned(k):
        wait(P2, k)
        par, par3 = lax.rem(k, 2), lax.rem(k, 3)
        return (rd[par3, cx, keep_a, :] + rp2[par, 0]) * scale, (rd[par3, 2 + cy, keep_b, :] + rp2[par, 1]) * scale

    @pl.when((step == 0) & (tile == 0))
    def _():
        pltpu.make_async_copy(q_ref, q_s, q_sem.at[0]).start()
        if full:
            pltpu.make_async_copy(wi_hbm.at[n_layers - 1], w_i, load_sem.at[0]).start()
            pltpu.make_async_copy(wo_hbm.at[n_layers - 1], w_o, load_sem.at[1]).start()
            greet([lax.rem(me + k + 1, 8) for k in range(7)])
            gath[me] = loss_ref[...]
            for copy in share_copies(me, gath, share_send, share_recv):
                copy.start()
        else:
            greet([mate, nx, ny])
            sq_out[...] = jnp.zeros_like(sq_out)
        pltpu.make_async_copy(q_ref, q_s, q_sem.at[0]).wait()

    if full:
        @pl.when((step == 1) & (tile == 0))
        def _():
            for copy in share_copies(me, gath, share_send, share_recv):
                copy.wait()
            loss_out[...] = jnp.full(loss_out.shape, 0.5 * (jnp.sum(gath[...]) * scale), F32)

    def start_pair(k):
        start(D2D, k)

    @pl.when(tile == 0)
    def _():
        when_layer(1, start_pair)
        if not full:
            when_layer(2, finish_p1)
        else:
            def keep_own(k):
                part_a, part_b = owned(k)
                par3 = lax.rem(k, 3)
                tot[par3, core, cx, keep_a, :] = part_a
                tot[par3, core, 2 + cy, keep_b, :] = part_b

            when_layer(2, keep_own)
            when_layer(1, finish_pair)

            def update_in(k):
                wait(GD, k)
                par3 = lax.rem(k, 3)
                pltpu.make_async_copy(wi_hbm.at[n_layers - 1 - k], w_i, load_sem.at[0]).wait()
                for blk in range(4):
                    cols = slice(blk * d, (blk + 1) * d)
                    w_i[:, cols] = w_i[:, cols] - LEARN_RATE * tot[par3, 0, blk]
                pltpu.make_async_copy(w_i, wi_new.at[n_layers - 1 - k], store_sem.at[0]).start()

            when_layer(4, update_in)

    @pl.when(tile == 1)
    def _():
        if not full:
            when_layer(1, finish_pair)
        else:
            def pass_on(k):
                wait(G2, k)
                start(G1, k)

            when_layer(3, pass_on)

            def update_out(k):
                par3 = lax.rem(k, 3)
                pltpu.make_async_copy(wo_hbm.at[n_layers - 1 - k], w_o, load_sem.at[1]).wait()
                for blk in range(4):
                    cols = slice(blk * d, (blk + 1) * d)
                    w_o[cols, :] = w_o[cols, :] - LEARN_RATE * tot[par3, 1, blk]
                pltpu.make_async_copy(w_o, wo_new.at[n_layers - 1 - k], store_sem.at[1]).start()

            when_layer(4, update_out)

    @pl.when(tile == 2)
    def _():
        if not full:
            def hand_out(k):
                par = lax.rem(k, 2)

                @pl.when(k >= 2)
                def _():
                    pltpu.make_async_copy(own.at[par], g_out.at[n_layers - 1 - k], own_sem.at[par]).wait()

                for j, part in enumerate(owned(k)):
                    own[par, j] = part
                    sq_out[...] += fold_rows(part, d)
                pltpu.make_async_copy(own.at[par], g_out.at[n_layers - 1 - k], own_sem.at[par]).start()

                @pl.when(k == n_layers - 1)
                def _():
                    pltpu.make_async_copy(own.at[1 - par], g_out.at[n_layers - 1 - k], own_sem.at[1 - par]).wait()
                    pltpu.make_async_copy(own.at[par], g_out.at[n_layers - 1 - k], own_sem.at[par]).wait()

            when_layer(2, hand_out)
        else:
            when_layer(1, finish_p1)

            def reload_in(k):
                pltpu.make_async_copy(w_i, wi_new.at[n_layers - 1 - k], store_sem.at[0]).wait()

                @pl.when(k < n_layers - 1)
                def _():
                    pltpu.make_async_copy(wi_hbm.at[n_layers - 2 - k], w_i, load_sem.at[0]).start()

            when_layer(4, reload_in)

    if full:
        @pl.when(tile == 3)
        def _():
            def cross(k):
                wait(G1, k)
                start(GD, k)

            when_layer(3, cross)
            when_layer(2, functools.partial(start, G2))

            def reload_out(k):
                pltpu.make_async_copy(w_o, wo_new.at[n_layers - 1 - k], store_sem.at[1]).wait()

                @pl.when(k < n_layers - 1)
                def _():
                    pltpu.make_async_copy(wo_hbm.at[n_layers - 2 - k], w_o, load_sem.at[1]).start()

            when_layer(4, reload_out)

    @pl.when(step < n_layers)
    def _():
        rows = pl.ds(tile * tok, tok)

        @pl.when(tile == 0)
        def _():
            acc_i[...] = jnp.zeros_like(acc_i)
            acc_o[...] = jnp.zeros_like(acc_o)

        q = q_s[rows, :]
        da = dot(q, vo_ref[0], 1, 1)
        act, slope = gelu_and_slope(z_ref[0].astype(F32))
        a_s[...] = act.astype(BF)
        p_s[...] = (da * slope).astype(BF)
        acc_i[...] += dot(h_ref[0], p_s[...], 0, 0)
        acc_o[...] += dot(q, a_s[...], 0, 0)
        back = dot(p_s[...], vi_ref[0], 1, 1)
        q_s[rows, :] = (q.astype(F32) + back).astype(BF)

        @pl.when(tile == N_TILES - 1)
        def _():
            for blk in range(4):
                cols = slice(blk * d, (blk + 1) * d)
                s_buf[0, blk] = acc_i[:, cols]
                s_buf[1, blk] = acc_o[:, cols].T


def solution(mesh):
    n_dev = mesh.shape["data"]

    def local_step(x_loc, y_loc, w_in, w_out):
        n_layers, d, ff = w_in.shape
        tokens = x_loc.shape[0] * x_loc.shape[1]
        tok = tokens // N_TILES
        scale = 1.0 / (tokens * n_dev * d)
        rho = RHO_FRAC * math.sqrt(n_layers * (d + ff))
        x_flat, y_flat = x_loc.reshape(tokens, d), y_loc.reshape(tokens, d)
        shape = jax.ShapeDtypeStruct
        dma, vmem = pltpu.SemaphoreType.DMA, pltpu.VMEM
        last = n_layers - 1
        tile_x = pl.BlockSpec((tok, d), lambda l, t: (jnp.where(l == 0, t, N_TILES - 1), 0))
        tile_y = pl.BlockSpec((tok, d), lambda l, t: (jnp.where(l == last, t, 0), 0))
        small = pl.BlockSpec((8, 128), lambda l, t: (0, 0))
        hbm = pl.BlockSpec(memory_space=ANY)

        def layer_of(rows, cols):
            return pl.BlockSpec((1, rows, cols), lambda l, t: (l, 0, 0))

        act_specs = [pl.BlockSpec((1, tok, ff), lambda l, t: (l, t, 0)), pl.BlockSpec((1, tok, d), lambda l, t: (l, t, 0)),
                     pl.BlockSpec((tokens, d), lambda l, t: (0, 0)), small, layer_of(d, ff), layer_of(ff, d)]
        act_shapes = [shape((n_layers, tokens, ff), BF), shape((n_layers, tokens, d), BF), shape((tokens, d), BF),
                      shape((8, 128), F32), shape((n_layers, d, ff), BF), shape((n_layers, ff, d), BF)]
        mul = 2 * tokens * d * ff * n_layers

        z_1, h_1, q_1, _, vi_1, vo_1 = pl.pallas_call(
            forward_kernel, name="forward", grid=(n_layers, N_TILES),
            in_specs=[tile_x, tile_y, layer_of(d, ff), layer_of(ff, d)],
            out_specs=act_specs, out_shape=act_shapes,
            scratch_shapes=[vmem((tokens, d), BF), vmem((tok, ff), BF)],
            cost_estimate=pl.CostEstimate(flops=2 * mul, bytes_accessed=10 ** 8, transcendentals=0),
            compiler_params=pltpu.CompilerParams(vmem_limit_bytes=VMEM_BYTES),
        )(x_flat, y_flat, w_in, w_out)

        def backward(full, q_0, z_all, h_all, vi, vo, *extra):
            n_steps = n_layers + (4 if full else 2)

            def at_layer(*block):
                def index(l, t):
                    live = l < n_layers
                    row = jnp.where(live, t, N_TILES - 1) if block[0] == tok else 0
                    return (jnp.maximum(last - l, 0), row, 0)
                return pl.BlockSpec((1,) + block, index)

            in_specs = [hbm, at_layer(tok, ff), at_layer(tok, d),
                        at_layer(d, ff), at_layer(ff, d)]
            scratch = [vmem((tokens, d), BF), vmem((d, ff), F32), vmem((d, ff), F32), vmem((tok, ff), BF), vmem((tok, ff), BF),
                       vmem((2, 4, d, d), F32), vmem((3, 4, d, d), F32), vmem((2, 2, d, d), F32), vmem((2, 2, d // 2, d), F32),
                       dma((6 if full else 3, 2, 2)), dma((6 if full else 3, 2, 2)), dma((1,))]
            if full:
                in_specs += [small, hbm, hbm]
                out_specs = [hbm, hbm, small]
                out_shape = [shape((n_layers, d, ff), F32), shape((n_layers, ff, d), F32), shape((8, 128), F32)]
                scratch += [vmem((3, 2, 4, d, d), F32), vmem((d, ff), F32), vmem((ff, d), F32), vmem((8, 8, 128), F32),
                            dma((7,)), dma((7,)), dma((2,)), dma((2,))]
            else:
                out_specs = [hbm, small]
                out_shape = [shape((n_layers, 2, d // 2, d), F32), shape((8, 128), F32)]
                scratch += [vmem((2, 2, d // 2, d), F32), dma((2,))]
            return pl.pallas_call(
                functools.partial(backward_kernel, full, n_layers, scale), name="backward_full" if full else "backward",
                grid=(n_steps, N_TILES), in_specs=in_specs, out_specs=out_specs, out_shape=out_shape, scratch_shapes=scratch,
                cost_estimate=pl.CostEstimate(flops=4 * mul, bytes_accessed=3 * 10 ** 8, transcendentals=0),
                compiler_params=pltpu.CompilerParams(vmem_limit_bytes=VMEM_BYTES, collective_id=2 if full else 0,
                                                     has_side_effects=True),
            )(q_0, z_all, h_all, vi, vo, *extra)

        g_own, sq_own = backward(False, q_1, z_1, h_1, vi_1, vo_1)

        z_2, h_2, q_2, loss_2, vi_2, vo_2 = pl.pallas_call(
            functools.partial(gather_kernel, n_layers, rho), name="gather_forward", grid=(n_layers, N_TILES),
            in_specs=[tile_x, tile_y, small, hbm, hbm, hbm],
            out_specs=act_specs, out_shape=act_shapes,
            scratch_shapes=[vmem((tokens, d), BF), vmem((tok, ff), BF), vmem((n_layers, 2, 4, d, d), BF),
                            vmem((n_layers, 2, d // 2, d), F32), vmem((n_layers, 2, d // 2, d), F32), vmem((8, 8, 128), F32),
                            dma((2,)), dma((7,)), dma((7,)), dma((3, 2, n_layers)), dma((3, 2, n_layers))],
            cost_estimate=pl.CostEstimate(flops=2 * mul, bytes_accessed=10 ** 8, transcendentals=0),
            compiler_params=pltpu.CompilerParams(vmem_limit_bytes=VMEM_BYTES, collective_id=1, has_side_effects=True),
        )(x_flat, y_flat, sq_own, g_own, w_in, w_out)

        new_in, new_out, loss = backward(True, q_2, z_2, h_2, vi_2, vo_2, loss_2, w_in, w_out)
        return new_in, new_out, loss[0, 0]

    return jax.shard_map(local_step, mesh=mesh, in_specs=(P("data"), P("data"), P(), P()), out_specs=(P(), P(), P()), check_vma=False)
```

time: 3470 us -> 1310 us (0.38)
  waiting for transfers between devices: 1860 us -> 0 us
  matrix products: 1340 us -> 0 us
  Pallas kernels: 0 us -> 1260 us
  other arithmetic: 158 us -> 0.01 us
  between operations: 39.7 us -> 0.71 us
    psum x2 -> x0, waiting for transfers between devices: 1860 us -> none  [the longest x1 941 us: local_step(): grad_in = [lax.psum(part_sum, 'data') * tok_scale for part_sum in sums_in]]
    dot_general x280 -> x0, matrix products: 1340 us -> none  [the longest x44 361 us: micro_grads(): jnp.einsum('bsd,fd->bsf', back_grad, wo_list[layer_idx], preferred_elemen...]
    pallas_call x0 -> x4, Pallas kernels: none -> 1260 us  [the longest x2 921 us: backward(): pl.pallas_call(functools.partial(backward_kernel, full, n_layers, scale),...]
    unnamed x56 -> x1, other arithmetic: 61.3 us -> 0.01 us
    convert_element_type x4 -> x0, other arithmetic: 49.3 us -> none  [the longest x2 25.4 us: local_step(): (w_in[layer_idx] + perturb_coef * grad_in[layer_idx]).astype(jnp.bfloat16)]
    reduce_sum x12 -> x0, other arithmetic: 41.8 us -> none  [local_step(): jnp.sum(grad_mat * grad_mat)]
  transfers between devices with their start and end apart: 2 -> 0, of which waited for: 2 -> 0; matrix products, arithmetic and copies ran while one was open for 0% -> 0% of each run, Pallas kernels for 0% -> 0%
where the time goes in v1:
time: 1310 us
  Pallas kernels  1260 us (96%)
  local copies, waits for them, and re-layouts  47.3 us (4%)
    pallas_call x2, Pallas kernels, backward(): pl.pallas_call(functools.partial(backward_kernel, full, n_layers, scale),...  921 us
    pallas_call x1, Pallas kernels, local_step(): pl.pallas_call(functools.partial(gather_kernel, n_layers, rho), name='gat...  184 us
    pallas_call x1, Pallas kernels, local_step(): pl.pallas_call(forward_kernel, name='forward', grid=(n_layers, N_TILES),...  158 us
    unnamed x18, local copies, waits for them, and re-layouts  41.8 us

profile of v1, /device:TPU:0, one launch (start us, length us, event | category | flops | bytes accessed | tf_op | source)
XLA Modules:
  0.0 1311.3 jit_solution(16347794113246774082)
XLA Ops:
  0.6 2.2 copy.9
  2.8 2.1 reshape.12.x_ref
  5.0 2.2 copy.10
  7.2 2.1 reshape.13.y_ref
  9.3 158.1 %forward.1 = (bf16[12,3136,1536]{2,1,0:T(8,128)(2,1)}, bf16[12,3136,384]{2,1,0:T(8,128)(2,1)}, bf16[3136,384]{1,0:T(8,128)(2,1)}, f32[8,128]{1,0:T(8,128)}, bf16...) custom-call(bf16[3136,384]{1,0:T(8,128)(2,1)} %reshape.12.x_ref, bf16[3136,384]{1,0:T(8,128)(2,1)} %reshape.13.y_ref, ...), custom_call_target="tpu_custom_call" | custom-call | flops 88785027072 | bytes 100000000 | tf_op jit(solution)/shard_map/forward/pallas_call | solution.py:480
  167.4 375.9 %backward.1 = (f32[12,2,192,384]{3,2,1,0:T(8,128)}, f32[8,128]{1,0:T(8,128)}) custom-call(bf16[3136,384]{1,0:T(8,128)(2,1)} %get-tuple-element.19.refs_0_, bf16[12,3136,1536]{2,1,0:T(8,128)(2,1)} %get-tuple-element.20.refs_1_, bf16[12,3136,384]{2,1,0:T(8,128)(2,1)} %get-tuple-element.21.refs_2_, bf16[12,384,1536]{2,1,0:T(8,128)(2,1)} %get-tuple-element.22.refs_3_, ...), custom_call_target="tpu_custom_call" | custom-call | flops 177570054144 | bytes 300000000 | tf_op jit(solution)/shard_map/backward/pallas_call | solution.py:514
  543.4 184.5 %gather_forward.1 = (bf16[12,3136,1536]{2,1,0:T(8,128)(2,1)}, bf16[12,3136,384]{2,1,0:T(8,128)(2,1)}, bf16[3136,384]{1,0:T(8,128)(2,1)}, f32[8,128]{1,0:T(8,128)...) custom-call(bf16[3136,384]{1,0:T(8,128)(2,1)} %reshape.12.x_ref, bf16[3136,384]{1,0:T(8,128)(2,1)} %reshape.13.y_ref, ...), custom_call_target="tpu_custom_call" | custom-call | flops 88785027072 | bytes 100000000 | tf_op jit(solution)/shard_map/gather_forward/pallas_call | solution.py:524
  727.8 544.9 %backward_full.1 = (f32[12,384,1536]{2,1,0:T(8,128)}, f32[12,1536,384]{2,1,0:T(8,128)}, f32[8,128]{1,0:T(8,128)}) custom-call(bf16[3136,384]{1,0:T(8,128)(2,1)} %get-tuple-element.26.refs_0_, bf16[12,3136,1536]{2,1,0:T(8,128)(2,1)} %get-tuple-element.27.refs_1_, bf16[12,3136,384]{2,1,0:T(8,128)(2,1)} %get-tuple-element.28.refs_2_, ...), custom_call_target="tpu_custom_call" | custom-call | flops 177570054144 | bytes 300000000 | tf_op jit(solution)/shard_map/backward_full/pallas_call | solution.py:514
  1272.7 1.2 slice.3
  1273.9 0.0 slice-start
  1273.9 0.0 slice-start.1
  1273.9 0.0 slice-start.2
  1273.9 0.0 slice-start.3
  1273.9 0.0 slice-start.4
  1273.9 0.0 slice-start.5
  1273.9 0.0 slice-start.6
  1273.9 23.8 %copy.13 = f32[12,384,1536]{2,1,0:T(8,128)} copy(f32[12,384,1536]{2,1,0:T(8,128)} %get-tuple-element.38) | data formatting | bytes 56623104
  1297.7 0.0 slice-done
  1297.7 0.0 slice-done.1
  1297.7 0.0 slice-done.2
  1297.8 0.0 slice-done.3
  1297.8 1.5 slice-done.4
  1299.3 1.2 slice-done.5
  1300.5 0.9 slice-done.6
  1301.4 10.0 copy.14
  (1 shorter events, 0.0 us)
Async XLA Ops:
  1273.9 23.9 %slice-start = ((s8[28311552]{0:T(1024)(128)(4,1)}), s8[4194304]{0:T(1024)(128)(4,1)S(1)}, s32[]{:S(2)}) async-start(s8[28311552]{0:T(1024)(128)(4,1)} %bitcast.1), calls=%async_computation | async-start | bytes 8388608
  1273.9 23.9 %slice-start.1 = ((s8[28311552]{0:T(1024)(128)(4,1)}), s8[4194304]{0:T(1024)(128)(4,1)S(1)}, s32[]{:S(2)}) async-start(s8[28311552]{0:T(1024)(128)(4,1)} %bitcast.1), calls=%async_computation.1 | async-start | bytes 8388608
  1273.9 23.9 %slice-start.2 = ((s8[28311552]{0:T(1024)(128)(4,1)}), s8[4194304]{0:T(1024)(128)(4,1)S(1)}, s32[]{:S(2)}) async-start(s8[28311552]{0:T(1024)(128)(4,1)} %bitcast.1), calls=%async_computation.2 | async-start | bytes 8388608
  1273.9 23.9 %slice-start.3 = ((s8[28311552]{0:T(1024)(128)(4,1)}), s8[4194304]{0:T(1024)(128)(4,1)S(1)}, s32[]{:S(2)}) async-start(s8[28311552]{0:T(1024)(128)(4,1)} %bitcast.1), calls=%async_computation.3 | async-start | bytes 8388608
  1273.9 25.4 %slice-start.4 = ((s8[28311552]{0:T(1024)(128)(4,1)}), s8[4194304]{0:T(1024)(128)(4,1)S(1)}, s32[]{:S(2)}) async-start(s8[28311552]{0:T(1024)(128)(4,1)} %bitcast.1), calls=%async_computation.4 | async-start | bytes 8388608
  1273.9 26.6 %slice-start.5 = ((s8[28311552]{0:T(1024)(128)(4,1)}), s8[4194304]{0:T(1024)(128)(4,1)S(1)}, s32[]{:S(2)}) async-start(s8[28311552]{0:T(1024)(128)(4,1)} %bitcast.1), calls=%async_computation.5 | async-start | bytes 8388608
  1273.9 27.5 %slice-start.6 = ((s8[28311552]{0:T(1024)(128)(4,1)}), s8[3145728]{0:T(1024)(128)(4,1)S(1)}, s32[]{:S(2)}) async-start(s8[28311552]{0:T(1024)(128)(4,1)} %bitcast.1), calls=%async_computation.6 | async-start | bytes 6291456
